TPU v7x, 32 devices: a whole 2x2x4 slice. The times are simulated.
32 devices in a mesh: date: 8 (over z, core), pix: 4 (over y, x).
Axes of the slice: x: 2, y: 2, z: 4, core: 2. Of those that a mesh axis runs over, the one named last changes fastest.
Arguments:
- bin_index: int32 [128, 262144], P('date', 'pix'), may hold values from 0 to 511
- clear_mask: bfloat16 [128, 262144], P('date', 'pix'), may hold values from 0 to 1, as said below
Outputs:
- anomaly: float32 [3, 2048], P(None, 'pix')
- tile_levels: float32 [3], replicated
Inputs may be any that keep to these rules, and one draw needn't show every extreme that they name: `clear_mask`: 0 for a cloudy observation, else a positive weight.
All inputs are finite; a program needn't handle non-finite values.
Results may differ from a plain program's by a relative error of at most 0.0003.
Values sent between devices are 32-bit elements; how exact they have to be, the bound alone decides.
No kernel may reach another device: no remote copies, remote signals or barrier semaphores. Data moves between devices by JAX's collectives and lax.ppermute only.
A program may use at most 64 MiB of HBM per device.

v0:
```python
import jax
import jax.numpy as jnp
from jax import lax
from jax.sharding import PartitionSpec as P

BINS = 512
BLOCK = 128
QUANTILES = (0.1, 0.5, 0.9)
LOW_EDGE = -1.0


def percentiles(counts, before, totals):
    target = jnp.stack([quantile * totals + 0.25 for quantile in QUANTILES])
    passed = jnp.clip(
        (target[:, :, None] - before[None]) / jnp.maximum(counts, 1.0)[None], 0.0, 1.0
    )
    return LOW_EDGE + 2.0 / BINS * jnp.sum(passed, axis=2)


def block_counts(bin_index, clear_mask, blocks):
    chosen = bin_index
    frames = chosen.shape[0]
    chosen = jnp.moveaxis(chosen.reshape(frames, blocks, BLOCK), 1, 0)
    weight = jnp.moveaxis(clear_mask.reshape(frames, blocks, BLOCK), 1, 0)
    upper_digit = chosen // 16
    lower_digit = chosen % 16
    upper_values = jnp.arange(BINS // 16, dtype=jnp.int32)
    lower_values = jnp.arange(16, dtype=jnp.int32)
    upper_table = jnp.where(
        upper_digit[:, None] == upper_values[None, :, None, None],
        weight[:, None],
        jnp.zeros((), jnp.bfloat16),
    )
    lower_table = (lower_digit[:, None] == lower_values[None, :, None, None]).astype(jnp.bfloat16)
    joint_counts = jnp.einsum(
        "ghdp,gldp->ghl", upper_table, lower_table, preferred_element_type=jnp.float32
    )
    return joint_counts.reshape(blocks, BINS)


def body(bin_index, clear_mask):
    date_devices = lax.axis_size("date")
    blocks_here = bin_index.shape[1] // BLOCK
    owned_rows = blocks_here // date_devices
    triangle = (jnp.arange(BINS)[:, None] < jnp.arange(BINS)[None, :]).astype(jnp.float32)
    owned_sums = lax.psum_scatter(
        block_counts(bin_index, clear_mask, owned_rows * lax.axis_size("date")),
        "date",
        scatter_dimension=0,
        tiled=True,
    )
    tile_counts = lax.psum(jnp.sum(owned_sums, axis=0), ("date", "pix"))
    tile_before = jnp.cumsum(tile_counts) - tile_counts
    tile_levels = percentiles(tile_counts[None], tile_before[None], jnp.sum(tile_counts)[None])[
        :, 0
    ]
    before = jnp.dot(owned_sums, triangle, precision=lax.Precision.HIGHEST)
    owned_levels = (
        percentiles(owned_sums, before, jnp.sum(owned_sums, axis=1)) - tile_levels[:, None]
    )
    anomaly = lax.all_gather(owned_levels, "date", axis=1, tiled=True)
    return (anomaly, tile_levels)


def solution(mesh):
    placed = (P("date", "pix"), P("date", "pix"))
    return jax.shard_map(
        body, mesh=mesh, in_specs=placed, out_specs=(P(None, "pix"), P()), check_vma=False
    )
```

profile of v0, /device:TPU:0, one launch (start us, length us, event | category | flops | bytes accessed | tf_op | source)
XLA Modules:
  0.0 145.4 jit_solution(10991119551946988317)
XLA Ops:
  7.2 0.0 reduce-scatter.4.cloned.1.call-start
  7.2 3.0 %copy.40 = s32[2,8,512,128]{3,2,1,0:T(8,128)S(1)} copy(s32[2,8,512,128]{3,1,2,0:T(8,128)} %bitcast.84) | data formatting | bytes 8388608
  10.2 3.8 %add_select_fusion.1 = (s32[512,16,128]{2,0,1:T(8,128)S(1)}, s32[512,16,128]{2,0,1:T(8,128)S(1)}) fusion(s32[2,8,512,128]{3,2,1,0:T(8,128)S(1)} %copy.40), kind=kLoop, calls=%fused_computation.9 | loop fusion | flops 19922944 | bytes 12582912 | tf_op jit(solution)/shard_map/jit(floor_divide)/jit(_where)/select_n | solution.py:25
  14.1 2.4 %copy.29 = s32[512,16,128]{2,1,0:T(8,128)S(1)} copy(s32[512,16,128]{2,0,1:T(8,128)S(1)} %get-tuple-element.4) | data formatting | bytes 8388608 | tf_op jit(solution)/shard_map/jit(floor_divide)/jit(_where)/select_n | solution.py:25
  16.5 0.0 copy-start
  16.5 2.4 %copy.31 = s32[512,16,128]{2,1,0:T(8,128)S(1)} copy(s32[512,16,128]{2,0,1:T(8,128)S(1)} %get-tuple-element.5) | data formatting | bytes 8388608 | tf_op jit(solution)/shard_map/jit(remainder)/select_n | solution.py:26
  18.9 0.0 copy-done
  19.0 0.4 copy.41
  19.3 1.4 copy.30
  20.7 20.1 %fusion.10 = f32[512,32,16]{1,2,0:T(8,128)} fusion(s32[512,16,128]{2,1,0:T(8,128)S(1)} %copy.31, s32[512,16,128]{2,1,0:T(8,128)S(1)} %copy.29, bf16[512,16,128]{2,1,0:T(8,128)(2,1)S(1)} %copy.30), kind=kOutput, calls=%fused_computation.18 | convolution fusion | flops 1157627904 | bytes 11534336 | tf_op jit(solution)/shard_map/ghdp,gldp->ghl/dot_general | solution.py:35
  40.8 3.2 %copy.32 = f32[512,32,16]{0,2,1:T(8,128)S(1)} copy(f32[512,32,16]{1,2,0:T(8,128)} %fusion.10) | data formatting | bytes 2097152 | tf_op jit(solution)/shard_map/ghdp,gldp->ghl/dot_general | solution.py:35
  44.0 1.3 copy.36
  45.4 0.0 reduce-scatter.4.cloned.1.call-update
  45.4 35.8 %reduce-scatter.4.cloned.1.call-done = f32[64,512]{1,0:T(8,128)} async-done(((f32[512,512]{1,0:T(8,128)}), f32[64,512]{1,0:T(8,128)}) %reduce-scatter.4.cloned.1.call-update) | async-done | bytes 131088
  81.2 1.0 fusion.15
  82.2 37.4 %psum.7 = f32[512]{0:T(512)S(1)} all-reduce(f32[512]{0:T(512)S(1)} %get-tuple-element.2), channel_id=1, replica_groups=mesh['date'=8,'pix'=4] {'date','pix'}, use_global_device_ids=true, to_apply=%region_4.5 | all-reduce | flops 512 | bytes 4096 | tf_op jit(solution)/shard_map/psum | solution.py:52
  119.6 0.3 reduce-window.9
  119.9 0.1 slice.7
  120.1 0.1 slice_reduce_fusion
  120.2 0.6 fusion.16
  122.7 0.1 maximum_bitcast_fusion
  122.8 0.2 clamp_reduce_fusion.1
  123.0 0.0 copy-start.1
  123.0 1.3 fusion.13
  124.3 0.2 clamp_reduce_fusion
  124.5 0.1 subtract_bitcast_fusion
  124.6 13.3 %all-gather = f32[8,64,3]{1,2,0:T(4,128)S(1)} all-gather(f32[1,64,3]{1,2,0:T(4,128)S(1)} %subtract_bitcast_fusion), channel_id=1, replica_groups=mesh['date'=8,'pix'=4] {'date'}, dimensions={0}, use_global_device_ids=true | all-gather | bytes 6912 | tf_op jit(solution)/shard_map/all_gather | solution.py:61
  137.9 0.7 reshape.186
  138.6 0.0 copy-done.1
  (5 shorter events, 0.1 us)
Async XLA Ops:
  7.2 74.0 %reduce-scatter.4.cloned.1.call-start = ((), (), s32[]{:S(2)}) async-start(), calls=%async_computation.1 | async-start | bytes 1179648
  16.5 2.5 %copy-start = (bf16[16,65536]{1,0:T(8,128)(2,1)S(1)}, bf16[16,65536]{1,0:T(8,128)(2,1)}, u32[]{:S(2)}) copy-start(bf16[16,65536]{1,0:T(8,128)(2,1)} %param.3) | copy-start | bytes 6291460
  123.0 15.6 %copy-start.1 = (f32[3]{0:T(128)}, f32[3]{0:T(128)S(1)}, u32[]{:S(2)}) copy-start(f32[3]{0:T(128)S(1)} %multiply_add_fusion) | copy-start | bytes 40
Sparse Core Ops, SparseCore 0:
  45.5 35.6 reduce-scatter.3
where the time goes:
time: 146 us; the launch traced here: 145 us
  blocking collectives  50.8 us (35%)
  waiting for transfers between devices  35.8 us (25%)
  matrix products  21.4 us (15%)
  between operations  16.1 us (11%)
  local copies, waits for them, and re-layouts  15 us (10%)
  other arithmetic  6.37 us (4%)
    psum x1, blocking collectives, body(): tile_counts = lax.psum(jnp.sum(owned_sums, axis=0), ('date', 'pix'))  37.4 us
    unnamed x2, waiting for transfers between devices  35.8 us
    dot_general x1, matrix products, block_counts(): jnp.einsum('ghdp,gldp->ghl', upper_table, lower_table, preferred_element_...  20.1 us
    all_gather x1, blocking collectives, body(): anomaly = lax.all_gather(owned_levels, 'date', axis=1, tiled=True)  13.3 us
    unnamed x8, local copies, waits for them, and re-layouts  5.39 us
    select_n x1, other arithmetic, block_counts(): upper_digit = chosen // 16  3.84 us
    dot_general x1, local copies, waits for them, and re-layouts, block_counts(): jnp.einsum('ghdp,gldp->ghl', upper_table, lower_table, preferred_element_...  3.23 us
  transfers between devices with their start and end apart: 1, of which 1 were waited for; matrix products, arithmetic and copies ran while one was open for 0% of the time, Pallas kernels for 0%

commit v1 on v0

--- a/solution.py
+++ b/solution.py
@@ -49,7 +49,8 @@
         scatter_dimension=0,
         tiled=True,
     )
-    tile_counts = lax.psum(jnp.sum(owned_sums, axis=0), ("date", "pix"))
+    one_axis = lax.psum(jnp.sum(owned_sums, axis=0), "pix")
+    tile_counts = lax.psum(one_axis, "date")
     tile_before = jnp.cumsum(tile_counts) - tile_counts
     tile_levels = percentiles(tile_counts[None], tile_before[None], jnp.sum(tile_counts)[None])[
         :, 0

time: 146 us -> 131 us (0.90)
  blocking collectives: 50.8 us -> 35.9 us
    psum x1 -> x2, blocking collectives: 37.4 us -> 23.1 us  [the longest x1 13.6 us: body(): tile_counts = lax.psum(one_axis, 'date')]
where the time goes in v1:
time: 131 us
  blocking collectives  35.9 us (27%)
  waiting for transfers between devices  35.8 us (27%)
  matrix products  21.4 us (16%)
  between operations  16.1 us (12%)
  local copies, waits for them, and re-layouts  15 us (11%)
  other arithmetic  6.37 us (5%)
    unnamed x2, waiting for transfers between devices  35.8 us
    dot_general x1, matrix products, block_counts(): jnp.einsum('ghdp,gldp->ghl', upper_table, lower_table, preferred_element_...  20.1 us
    psum x1, blocking collectives, body(): tile_counts = lax.psum(one_axis, 'date')  13.6 us
    all_gather x1, blocking collectives, body(): anomaly = lax.all_gather(owned_levels, 'date', axis=1, tiled=True)  12.8 us
    psum x1, blocking collectives, body(): one_axis = lax.psum(jnp.sum(owned_sums, axis=0), 'pix')  9.51 us
    unnamed x8, local copies, waits for them, and re-layouts  5.39 us
    select_n x1, other arithmetic, block_counts(): upper_digit = chosen // 16  3.84 us
    dot_general x1, local copies, waits for them, and re-layouts, block_counts(): jnp.einsum('ghdp,gldp->ghl', upper_table, lower_table, preferred_element_...  3.23 us
  transfers between devices with their start and end apart: 1, of which 1 were waited for; matrix products, arithmetic and copies ran while one was open for 0% of the time, Pallas kernels for 0%

profile of v1, /device:TPU:0, one launch (start us, length us, event | category | flops | bytes accessed | tf_op | source)
XLA Modules:
  0.0 130.5 jit_solution(15436058891425254221)
XLA Ops:
  7.2 0.0 reduce-scatter.4.cloned.1.call-start
  7.2 3.0 %copy.40 = s32[2,8,512,128]{3,2,1,0:T(8,128)S(1)} copy(s32[2,8,512,128]{3,1,2,0:T(8,128)} %bitcast.84) | data formatting | bytes 8388608
  10.2 3.8 %add_select_fusion.1 = (s32[512,16,128]{2,0,1:T(8,128)S(1)}, s32[512,16,128]{2,0,1:T(8,128)S(1)}) fusion(s32[2,8,512,128]{3,2,1,0:T(8,128)S(1)} %copy.40), kind=kLoop, calls=%fused_computation.9 | loop fusion | flops 19922944 | bytes 12582912 | tf_op jit(solution)/shard_map/jit(floor_divide)/jit(_where)/select_n | solution.py:25
  14.1 2.4 %copy.29 = s32[512,16,128]{2,1,0:T(8,128)S(1)} copy(s32[512,16,128]{2,0,1:T(8,128)S(1)} %get-tuple-element.4) | data formatting | bytes 8388608 | tf_op jit(solution)/shard_map/jit(floor_divide)/jit(_where)/select_n | solution.py:25
  16.5 0.0 copy-start
  16.5 2.4 %copy.31 = s32[512,16,128]{2,1,0:T(8,128)S(1)} copy(s32[512,16,128]{2,0,1:T(8,128)S(1)} %get-tuple-element.5) | data formatting | bytes 8388608 | tf_op jit(solution)/shard_map/jit(remainder)/select_n | solution.py:26
  18.9 0.0 copy-done
  19.0 0.4 copy.41
  19.3 1.4 %copy.30 = bf16[512,16,128]{2,1,0:T(8,128)(2,1)S(1)} copy(bf16[512,16,128]{2,0,1:T(8,128)(2,1)S(1)} %bitcast.82) | data formatting | bytes 4194304 | tf_op jit(solution)/shard_map/transpose | solution.py:24
  20.7 20.1 %fusion.10 = f32[512,32,16]{1,2,0:T(8,128)} fusion(s32[512,16,128]{2,1,0:T(8,128)S(1)} %copy.31, s32[512,16,128]{2,1,0:T(8,128)S(1)} %copy.29, bf16[512,16,128]{2,1,0:T(8,128)(2,1)S(1)} %copy.30), kind=kOutput, calls=%fused_computation.18 | convolution fusion | flops 1157627904 | bytes 11534336 | tf_op jit(solution)/shard_map/ghdp,gldp->ghl/dot_general | solution.py:35
  40.8 3.2 %copy.32 = f32[512,32,16]{0,2,1:T(8,128)S(1)} copy(f32[512,32,16]{1,2,0:T(8,128)} %fusion.10) | data formatting | bytes 2097152 | tf_op jit(solution)/shard_map/ghdp,gldp->ghl/dot_general | solution.py:35
  44.0 1.3 %copy.36 = f32[512,512]{1,0:T(8,128)} copy(f32[512,512]{0,1:T(8,128)S(1)} %bitcast.83) | data formatting | bytes 2097152
  45.4 0.0 reduce-scatter.4.cloned.1.call-update
  45.4 35.8 %reduce-scatter.4.cloned.1.call-done = f32[64,512]{1,0:T(8,128)} async-done(((f32[512,512]{1,0:T(8,128)}), f32[64,512]{1,0:T(8,128)}) %reduce-scatter.4.cloned.1.call-update) | async-done | bytes 131088
  81.2 1.0 fusion.15
  82.2 9.5 %psum.14 = f32[512]{0:T(512)S(1)} all-reduce(f32[512]{0:T(512)S(1)} %get-tuple-element.2), channel_id=1, replica_groups=mesh['date'=8,'pix'=4] {'pix'}, use_global_device_ids=true, to_apply=%region_4.5 | all-reduce | flops 512 | bytes 4096 | tf_op jit(solution)/shard_map/psum | solution.py:52
  91.7 13.6 %psum.15 = f32[512]{0:T(512)S(1)} all-reduce(f32[512]{0:T(512)S(1)} %psum.14), channel_id=1, replica_groups=mesh['date'=8,'pix'=4] {'date'}, use_global_device_ids=true, to_apply=%region_5.6 | all-reduce | flops 512 | bytes 4096 | tf_op jit(solution)/shard_map/psum | solution.py:53
  105.3 0.3 reduce-window.9
  105.6 0.1 slice.7
  105.7 0.1 slice_reduce_fusion
  105.8 0.6 fusion.16
  108.4 0.1 maximum_bitcast_fusion
  108.5 0.2 clamp_reduce_fusion.1
  108.6 0.0 copy-start.1
  108.7 1.3 fusion.13
  109.9 0.2 clamp_reduce_fusion
  110.1 0.1 subtract_bitcast_fusion
  110.2 12.8 %all-gather = f32[8,64,3]{1,2,0:T(4,128)S(1)} all-gather(f32[1,64,3]{1,2,0:T(4,128)S(1)} %subtract_bitcast_fusion), channel_id=1, replica_groups=mesh['date'=8,'pix'=4] {'date'}, dimensions={0}, use_global_device_ids=true | all-gather | bytes 6912 | tf_op jit(solution)/shard_map/all_gather | solution.py:62
  123.0 0.7 reshape.186
  123.7 0.0 copy-done.1
  (5 shorter events, 0.1 us)
Async XLA Ops:
  7.2 74.0 %reduce-scatter.4.cloned.1.call-start = ((), (), s32[]{:S(2)}) async-start(), calls=%async_computation.1 | async-start | bytes 1179648
  16.5 2.5 %copy-start = (bf16[16,65536]{1,0:T(8,128)(2,1)S(1)}, bf16[16,65536]{1,0:T(8,128)(2,1)}, u32[]{:S(2)}) copy-start(bf16[16,65536]{1,0:T(8,128)(2,1)} %param.3) | copy-start | bytes 6291460
  108.6 15.0 %copy-start.1 = (f32[3]{0:T(128)}, f32[3]{0:T(128)S(1)}, u32[]{:S(2)}) copy-start(f32[3]{0:T(128)S(1)} %multiply_add_fusion) | copy-start | bytes 40
Sparse Core Ops, SparseCore 0:
  45.5 35.6 reduce-scatter.3

commit v2 on v0

--- a/solution.py
+++ b/solution.py
@@ -49,7 +49,9 @@
         scatter_dimension=0,
         tiled=True,
     )
-    tile_counts = lax.psum(jnp.sum(owned_sums, axis=0), ("date", "pix"))
+    x = jnp.sum(owned_sums, axis=0)
+    pieces = lax.all_gather(x, ("date", "pix"))
+    tile_counts = jnp.sum(pieces, axis=0)
     tile_before = jnp.cumsum(tile_counts) - tile_counts
     tile_levels = percentiles(tile_counts[None], tile_before[None], jnp.sum(tile_counts)[None])[
         :, 0

time: 146 us -> 174 us (1.19)
  blocking collectives: 50.8 us -> 78.5 us
    all_gather x0 -> x1, blocking collectives: none -> 65.7 us  [body(): pieces = lax.all_gather(x, ('date', 'pix'))]
    psum x1 -> x0, blocking collectives: 37.4 us -> none  [body(): tile_counts = lax.psum(jnp.sum(owned_sums, axis=0), ('date', 'pix'))]
where the time goes in v2:
time: 174 us; the launch traced here: 173 us
  blocking collectives  78.5 us (45%)
  waiting for transfers between devices  35.8 us (21%)
  matrix products  21.4 us (12%)
  between operations  16.1 us (9%)
  local copies, waits for them, and re-layouts  15 us (9%)
  other arithmetic  6.57 us (4%)
    all_gather x1, blocking collectives, body(): pieces = lax.all_gather(x, ('date', 'pix'))  65.7 us
    unnamed x2, waiting for transfers between devices  35.8 us
    dot_general x1, matrix products, block_counts(): jnp.einsum('ghdp,gldp->ghl', upper_table, lower_table, preferred_element_...  20.1 us
    all_gather x1, blocking collectives, body(): anomaly = lax.all_gather(owned_levels, 'date', axis=1, tiled=True)  12.8 us
    unnamed x8, local copies, waits for them, and re-layouts  5.39 us
    select_n x1, other arithmetic, block_counts(): upper_digit = chosen // 16  3.84 us
  transfers between devices with their start and end apart: 1, of which 1 were waited for; matrix products, arithmetic and copies ran while one was open for 0% of the time, Pallas kernels for 0%

profile of v2, /device:TPU:0, one launch (start us, length us, event | category | flops | bytes accessed | tf_op | source)
XLA Modules:
  0.0 173.4 jit_solution(3031015748234337034)
XLA Ops:
  7.2 0.0 reduce-scatter.4.cloned.1.call-start
  7.2 3.0 %copy.40 = s32[2,8,512,128]{3,2,1,0:T(8,128)S(1)} copy(s32[2,8,512,128]{3,1,2,0:T(8,128)} %bitcast.85) | data formatting | bytes 8388608
  10.2 3.8 %add_select_fusion.1 = (s32[512,16,128]{2,0,1:T(8,128)S(1)}, s32[512,16,128]{2,0,1:T(8,128)S(1)}) fusion(s32[2,8,512,128]{3,2,1,0:T(8,128)S(1)} %copy.40), kind=kLoop, calls=%fused_computation.9 | loop fusion | flops 19922944 | bytes 12582912 | tf_op jit(solution)/shard_map/jit(floor_divide)/jit(_where)/select_n | solution.py:25
  14.1 2.4 %copy.29 = s32[512,16,128]{2,1,0:T(8,128)S(1)} copy(s32[512,16,128]{2,0,1:T(8,128)S(1)} %get-tuple-element.6) | data formatting | bytes 8388608 | tf_op jit(solution)/shard_map/jit(floor_divide)/jit(_where)/select_n | solution.py:25
  16.5 0.0 copy-start
  16.5 2.4 %copy.31 = s32[512,16,128]{2,1,0:T(8,128)S(1)} copy(s32[512,16,128]{2,0,1:T(8,128)S(1)} %get-tuple-element.7) | data formatting | bytes 8388608 | tf_op jit(solution)/shard_map/jit(remainder)/select_n | solution.py:26
  18.9 0.0 copy-done
  19.0 0.4 copy.41
  19.3 1.4 copy.30
  20.7 20.1 %fusion.10 = f32[512,32,16]{1,2,0:T(8,128)} fusion(s32[512,16,128]{2,1,0:T(8,128)S(1)} %copy.31, s32[512,16,128]{2,1,0:T(8,128)S(1)} %copy.29, bf16[512,16,128]{2,1,0:T(8,128)(2,1)S(1)} %copy.30), kind=kOutput, calls=%fused_computation.18 | convolution fusion | flops 1157627904 | bytes 11534336 | tf_op jit(solution)/shard_map/ghdp,gldp->ghl/dot_general | solution.py:35
  40.8 3.2 %copy.32 = f32[512,32,16]{0,2,1:T(8,128)S(1)} copy(f32[512,32,16]{1,2,0:T(8,128)} %fusion.10) | data formatting | bytes 2097152 | tf_op jit(solution)/shard_map/ghdp,gldp->ghl/dot_general | solution.py:35
  44.0 1.3 copy.36
  45.4 0.0 reduce-scatter.4.cloned.1.call-update
  45.4 35.8 %reduce-scatter.4.cloned.1.call-done = f32[64,512]{1,0:T(8,128)} async-done(((f32[512,512]{1,0:T(8,128)}), f32[64,512]{1,0:T(8,128)}) %reduce-scatter.4.cloned.1.call-update) | async-done | bytes 131088
  81.2 1.0 fusion.15
  82.2 65.7 %all-gather.1 = f32[32,1,512]{2,1,0:T(1,128)S(1)} all-gather(f32[1,1,512]{2,1,0:T(1,128)S(1)} %bitcast.88), channel_id=2, replica_groups=mesh['date'=8,'pix'=4] {'date','pix'}, dimensions={0}, use_global_device_ids=true | all-gather | bytes 67584 | tf_op jit(solution)/shard_map/all_gather | solution.py:53
  147.9 0.7 fusion.16
  150.6 0.3 reduce-window.9
  150.9 0.1 slice.7
  151.0 0.1 slice_reduce_fusion
  151.1 0.1 bitcast_subtract_fusion
  151.2 0.1 maximum_bitcast_fusion
  151.3 0.2 clamp_reduce_fusion.1
  151.5 0.0 copy-start.1
  151.5 1.3 fusion.13
  152.8 0.2 clamp_reduce_fusion
  153.0 0.1 subtract_bitcast_fusion
  153.1 12.8 %all-gather.2 = f32[8,64,3]{1,2,0:T(4,128)S(1)} all-gather(f32[1,64,3]{1,2,0:T(4,128)S(1)} %subtract_bitcast_fusion), channel_id=1, replica_groups=mesh['date'=8,'pix'=4] {'date'}, dimensions={0}, use_global_device_ids=true | all-gather | bytes 6912 | tf_op jit(solution)/shard_map/all_gather | solution.py:63
  165.8 0.7 reshape.206
  166.5 0.0 copy-done.1
  (5 shorter events, 0.1 us)
Async XLA Ops:
  7.2 74.0 %reduce-scatter.4.cloned.1.call-start = ((), (), s32[]{:S(2)}) async-start(), calls=%async_computation.1 | async-start | bytes 1179648
  16.5 2.5 %copy-start = (bf16[16,65536]{1,0:T(8,128)(2,1)S(1)}, bf16[16,65536]{1,0:T(8,128)(2,1)}, u32[]{:S(2)}) copy-start(bf16[16,65536]{1,0:T(8,128)(2,1)} %param.3) | copy-start | bytes 6291460
  151.5 15.0 %copy-start.1 = (f32[3]{0:T(128)}, f32[3]{0:T(128)S(1)}, u32[]{:S(2)}) copy-start(f32[3]{0:T(128)S(1)} %multiply_add_fusion) | copy-start | bytes 40
Sparse Core Ops, SparseCore 0:
  45.5 35.6 reduce-scatter.3
